TPU v7x, 32 devices: a whole 2x2x4 slice. The times are simulated.
32 devices in a mesh: dp: 4 (over x, core), section: 2 (over y), tensor: 4 (over z).
Axes of the slice: x: 2, y: 2, z: 4, core: 2. Of those that a mesh axis runs over, the one named last changes fastest.
Arguments:
- observed: float32 [4, 2, 4, 2646], P('dp', 'section', 'tensor'), may hold values from 0.25 to 8
- section_of: int32 [126], replicated, may hold values from 0 to 1, as said below
- hist_len: int32 [21], replicated, may hold values from 1 to 127
- roll_index: int32 [], replicated, may hold values from 0 to 127
- history: float32 [128, 2646], replicated, may hold values from 0.02 to 64
- acts: bfloat16 [2, 1536, 16384], P('section', 'dp', 'tensor'), may hold values from -6 to 6
- grads: bfloat16 [2, 1536, 1024], P('section', 'dp', 'tensor'), may hold values from -6 to 6
Outputs:
- new_history: float32 [128, 2646], replicated
- new_scale: float32 [2646], replicated
- wgrad: bfloat16 [2, 16384, 1024], P('section', ('tensor', 'dp'))
Inputs may be any that keep to these rules, and one draw needn't show every extreme that they name: `section_of`: layers are assigned to sections in contiguous ascending groups, and every section holds at least one layer.
All inputs are finite; a program needn't handle non-finite values.
Results may differ from a plain program's by a relative error of at most 0.017.
Values may be sent and summed in bfloat16 or wider, within the bound.
A program may use at most 64 MiB of HBM per device.

v0:
```python
import jax
import jax.numpy as jnp
from jax import lax
from jax.sharding import PartitionSpec as P

FP8_MAX = 448.0


def merge_amax(local):
    merged = lax.pmax(local, "tensor")
    merged = lax.pmax(merged, "section")
    return lax.pmax(merged, "dp")


def weight_grad(acts, grads, scale_x, scale_g):
    denom = scale_x * scale_g
    acts_q = jnp.clip(acts[0].astype(jnp.float32) * scale_x, -FP8_MAX, FP8_MAX).astype(jnp.bfloat16)
    grads_q = jnp.clip(grads[0].astype(jnp.float32) * scale_g, -FP8_MAX, FP8_MAX).astype(
        jnp.bfloat16
    )
    grads_all = lax.all_gather(grads_q, "tensor", axis=1, tiled=True)
    product = lax.dot_general(
        acts_q, grads_all, (((0,), (0,)), ((), ())), preferred_element_type=jnp.float32
    )
    summed = lax.psum_scatter(
        (product / denom).astype(jnp.bfloat16), "dp", scatter_dimension=0, tiled=True
    )
    return summed[None]


def body(observed, section_of, hist_len, roll_index, history, acts, grads):
    section = lax.axis_index("section")
    kinds = hist_len.shape[0]
    total_tensors = history.shape[1]
    slot_count = history.shape[0]
    kind_len = jnp.tile(hist_len, total_tensors // kinds)
    slots = lax.broadcasted_iota(jnp.int32, (slot_count, 1), 0)
    age = (roll_index - slots) % slot_count
    first = jnp.sum((section_of < section).astype(jnp.int32))
    columns = lax.dynamic_slice_in_dim(history, first * kinds, 2, 1)
    pair_len = hist_len[:2]
    old_window = (age >= 1) & (age <= pair_len[None, :])
    old_scale = FP8_MAX / jnp.max(jnp.where(old_window, columns, jnp.float32(0.0)), axis=0)
    owned = jnp.repeat(section_of == section, kinds)
    local = jnp.where(owned, observed.reshape(total_tensors), jnp.float32(0.0))
    merged = merge_amax(local)
    wgrad = weight_grad(acts, grads, old_scale[0], old_scale[1])
    new_history = jnp.where(slots == roll_index, merged[None, :], history)
    new_window = age < kind_len[None, :]
    new_scale = FP8_MAX / jnp.max(jnp.where(new_window, new_history, jnp.float32(0.0)), axis=0)
    return (new_history, new_scale, wgrad)


def solution(mesh):
    in_specs = (
        P("dp", "section", "tensor", None),
        P(),
        P(),
        P(),
        P(),
        P("section", "dp", "tensor"),
        P("section", "dp", "tensor"),
    )
    out_specs = (P(), P(), P("section", ("tensor", "dp"), None))
    return jax.shard_map(body, mesh=mesh, in_specs=in_specs, out_specs=out_specs, check_vma=False)
```

profile of v0, /device:TPU:0, one launch (start us, length us, event | category | flops | bytes accessed | tf_op | source)
XLA Modules:
  0.0 123.1 jit_solution(12922742336281192124)
XLA Ops:
  7.2 0.0 reduce-scatter.2.cloned.1.call-start
  7.9 1.3 %fusion.7 = s32[]{:T(128)} fusion(s32[126]{0:T(128)} %param.8, s32[]{:T(128)S(6)} %axis_index.15), kind=kLoop, calls=%fused_computation.18 | loop fusion | flops 377 | bytes 512 | tf_op jit(solution)/shard_map/reduce_sum | solution.py:39
  9.8 0.9 fusion.6
  10.7 0.6 fusion.11
  12.6 1.6 %clamp_convert_fusion.1 = bf16[1,384,256]{2,1,0:T(8,128)(2,1)S(1)} fusion(bf16[1,384,256]{2,1,0:T(8,128)(2,1)} %param.13, f32[]{:T(128)} %bitcast.2), kind=kLoop, calls=%fused_computation.9 | loop fusion | flops 393216 | bytes 393220 | tf_op jit(solution)/shard_map/convert_element_type | solution.py:18
  14.3 21.3 %all-gather = bf16[1,384,1024]{2,1,0:T(8,128)(2,1)S(1)} all-gather(bf16[1,384,256]{2,1,0:T(8,128)(2,1)S(1)} %clamp_convert_fusion.1), channel_id=2, replica_groups=mesh['dp'=4,'section'=2,'tensor'=4] {'tensor'}, dimensions={2}, use_global_device_ids=true | all-gather | bytes 983040 | tf_op jit(solution)/shard_map/all_gather | solution.py:21
  35.6 9.5 %divide_convert_fusion = bf16[4096,1024]{1,0:T(8,128)(2,1)} fusion(f32[]{:T(128)S(6)} %mul.25, bf16[1,384,4096]{2,1,0:T(8,128)(2,1)} %param.12, f32[]{:T(128)} %bitcast, bf16[1,384,1024]{2,1,0:T(8,128)(2,1)S(1)} %all-gather), kind=kOutput, calls=%fused_computation | convolution fusion | flops 3235905536 | bytes 12320776 | tf_op jit(solution)/shard_map/dot_general | solution.py:22
  45.0 0.0 copy-start.3
  45.0 0.0 copy-start.2
  45.0 0.0 copy-start.1
  45.0 0.0 copy-start
  45.0 0.0 reduce-scatter.2.cloned.1.call-update
  45.1 0.6 copy-done.3
  45.7 0.1 broadcast_in_dim.37
  45.8 0.2 reshape.60
  46.0 0.0 copy-done.2
  46.0 0.2 lt.30
  46.2 0.0 copy-done.1
  46.3 17.1 %pmax.21 = f32[2646]{0:T(1024)S(1)} all-reduce(f32[2646]{0:T(1024)S(1)} %broadcast_select_fusion.1), channel_id=1, replica_groups=mesh['dp'=4,'section'=2,'tensor'=4] {'tensor'}, use_global_device_ids=true, to_apply=%region_0.1 | all-reduce | flops 2646 | bytes 21168 | tf_op jit(solution)/shard_map/pmax | solution.py:10
  63.3 8.1 %pmax.22 = f32[2646]{0:T(1024)S(1)} all-reduce(f32[2646]{0:T(1024)S(1)} %pmax.21), channel_id=1, replica_groups=mesh['dp'=4,'section'=2,'tensor'=4] {'section'}, use_global_device_ids=true, to_apply=%region_1.2 | all-reduce | flops 2646 | bytes 21168 | tf_op jit(solution)/shard_map/pmax | solution.py:11
  71.4 11.8 %pmax.23 = f32[2646]{0:T(1024)S(1)} all-reduce(f32[2646]{0:T(1024)S(1)} %pmax.22), channel_id=1, replica_groups=mesh['dp'=4,'section'=2,'tensor'=4] {'dp'}, use_global_device_ids=true, to_apply=%region_2.3 | all-reduce | flops 2646 | bytes 21168 | tf_op jit(solution)/shard_map/pmax | solution.py:12
  83.2 0.0 copy-done
  83.2 2.9 %select_reduce_fusion = (f32[2646]{0:T(1024)S(1)}, f32[128,2646]{0,1:T(8,128)}) fusion(s32[128]{0:T(128)S(1)} %and_select_fusion.1, s32[2646]{0:T(1024)S(1)} %lt.30, f32[128,2646]{0,1:T(8,128)S(1)} %copy-done, f32[2646]{0:T(1024)S(1)} %pmax.23, pred[128]{0:T(512)(128)(4,1)S(1)} %iota_compare_fusion), kind=kLoop, calls=%fused_computation.6 | loop fusion | flops 1352106 | bytes 2741896 | tf_op jit(solution)/shard_map/reduce_max | solution.py:50
  86.1 0.6 broadcast_divide_fusion
  86.7 29.6 %reduce-scatter.2.cloned.1.call-done = bf16[1024,1024]{1,0:T(8,128)(2,1)} async-done(((bf16[4096,1024]{1,0:T(8,128)(2,1)}), bf16[1024,1024]{1,0:T(8,128)(2,1)}) %reduce-scatter.2.cloned.1.call-update) | async-done | bytes 2097168 | tf_op jit(solution)/shard_map/reduce_scatter | solution.py:25
  (8 shorter events, 0.1 us)
Async XLA Ops:
  7.2 109.1 %reduce-scatter.2.cloned.1.call-start = ((), (), s32[]{:S(2)}) async-start(), calls=%async_computation.1 | async-start | bytes 10485760 | tf_op jit(solution)/shard_map/reduce_scatter | solution.py:25
  45.0 0.7 copy-start.3
  45.0 1.0 copy-start.2
  45.0 1.2 copy-start.1
  45.0 38.2 %copy-start = (f32[128,2646]{0,1:T(8,128)S(1)}, f32[128,2646]{0,1:T(8,128)}, u32[]{:S(2)}) copy-start(f32[128,2646]{0,1:T(8,128)} %param.11) | copy-start | bytes 4064260
Sparse Core Ops, SparseCore 0:
  45.2 70.9 reduce-scatter.1
where the time goes:
time: 123 us
  blocking collectives  58.2 us (47%)
  waiting for transfers between devices  29.6 us (24%)
  between operations  16.7 us (14%)
  matrix products  9.46 us (8%)
  other arithmetic  7.36 us (6%)
  local copies, waits for them, and re-layouts  1.72 us (1%)
    reduce_scatter x1, waiting for transfers between devices, weight_grad(): lax.psum_scatter((product / denom).astype(jnp.bfloat16), 'dp', scatter_di...  29.6 us
    all_gather x1, blocking collectives, weight_grad(): grads_all = lax.all_gather(grads_q, 'tensor', axis=1, tiled=True)  21.3 us
    pmax x1, blocking collectives, merge_amax(): merged = lax.pmax(local, 'tensor')  17.1 us
    pmax x1, blocking collectives, merge_amax(): return lax.pmax(merged, 'dp')  11.8 us
    dot_general x1, matrix products, weight_grad(): lax.dot_general(acts_q, grads_all, (((0,), (0,)), ((), ())), preferred_el...  9.46 us
    pmax x1, blocking collectives, merge_amax(): merged = lax.pmax(merged, 'section')  8.09 us
    reduce_max x1, other arithmetic, body(): jnp.max(jnp.where(new_window, new_history, jnp.float32(0.0)), axis=0)  2.87 us
  transfers between devices with their start and end apart: 1, of which 1 were waited for; matrix products, arithmetic and copies ran while one was open for 3% of the time, Pallas kernels for 0%

commit v1 on v0

--- a/solution.py
+++ b/solution.py
@@ -18,7 +18,7 @@
     grads_q = jnp.clip(grads[0].astype(jnp.float32) * scale_g, -FP8_MAX, FP8_MAX).astype(
         jnp.bfloat16
     )
-    grads_all = lax.all_gather(grads_q, "tensor", axis=1, tiled=True)
+    grads_all = jnp.concatenate(lax.all_gather(grads_q, "tensor"), axis=1)
     product = lax.dot_general(
         acts_q, grads_all, (((0,), (0,)), ((), ())), preferred_element_type=jnp.float32
     )

time: 123 us -> 124 us (level)
  no operation moved by 1% of the time
where the time goes in v1:
time: 124 us; the launch traced here: 123 us
  blocking collectives  58.2 us (47%)
  waiting for transfers between devices  29.6 us (24%)
  between operations  16.7 us (13%)
  matrix products  9.48 us (8%)
  other arithmetic  7.36 us (6%)
  local copies, waits for them, and re-layouts  2.08 us (2%)
    reduce_scatter x1, waiting for transfers between devices, weight_grad(): lax.psum_scatter((product / denom).astype(jnp.bfloat16), 'dp', scatter_di...  29.6 us
    all_gather x1, blocking collectives, weight_grad(): grads_all = jnp.concatenate(lax.all_gather(grads_q, 'tensor'), axis=1)  21.3 us
    pmax x1, blocking collectives, merge_amax(): merged = lax.pmax(local, 'tensor')  17 us
    pmax x1, blocking collectives, merge_amax(): return lax.pmax(merged, 'dp')  11.8 us
    dot_general x1, matrix products, weight_grad(): lax.dot_general(acts_q, grads_all, (((0,), (0,)), ((), ())), preferred_el...  9.48 us
    pmax x1, blocking collectives, merge_amax(): merged = lax.pmax(merged, 'section')  8.09 us
    reduce_max x1, other arithmetic, body(): jnp.max(jnp.where(new_window, new_history, jnp.float32(0.0)), axis=0)  2.87 us
  transfers between devices with their start and end apart: 1, of which 1 were waited for; matrix products, arithmetic and copies ran while one was open for 3% of the time, Pallas kernels for 0%

profile of v1, /device:TPU:0, one launch (start us, length us, event | category | flops | bytes accessed | tf_op | source)
XLA Modules:
  0.0 123.5 jit_solution(8110476038743317213)
XLA Ops:
  7.2 0.0 reduce-scatter.2.cloned.1.call-start
  7.9 1.3 %fusion.6 = s32[]{:T(128)} fusion(s32[126]{0:T(128)} %param.8, s32[]{:T(128)S(6)} %axis_index.15), kind=kLoop, calls=%fused_computation.17 | loop fusion | flops 377 | bytes 512 | tf_op jit(solution)/shard_map/reduce_sum | solution.py:39
  9.8 0.9 fusion.5
  10.7 0.6 fusion.10
  12.6 1.6 %clamp_convert_fusion.1 = bf16[1,384,256]{2,1,0:T(8,128)(2,1)S(1)} fusion(bf16[1,384,256]{2,1,0:T(8,128)(2,1)} %param.13, f32[]{:T(128)} %bitcast.2), kind=kLoop, calls=%fused_computation.8 | loop fusion | flops 393216 | bytes 393220 | tf_op jit(solution)/shard_map/convert_element_type | solution.py:18
  14.3 21.3 %all_gather.4 = bf16[4,384,256]{2,1,0:T(8,128)(2,1)S(1)} all-gather(bf16[1,384,256]{2,1,0:T(8,128)(2,1)S(1)} %clamp_convert_fusion.1), channel_id=1, replica_groups=mesh['dp'=4,'section'=2,'tensor'=4] {'tensor'}, dimensions={0}, use_global_device_ids=true | all-gather | bytes 983040 | tf_op jit(solution)/shard_map/all_gather | solution.py:21
  35.6 0.4 copy.11
  35.9 9.5 %divide_convert_fusion = bf16[4096,1024]{1,0:T(8,128)(2,1)} fusion(f32[]{:T(128)S(6)} %mul.25, bf16[384,1024]{0,1:T(8,128)(2,1)S(1)} %bitcast.11, bf16[1,384,4096]{2,1,0:T(8,128)(2,1)} %param.12, f32[]{:T(128)} %bitcast), kind=kOutput, calls=%fused_computation | convolution fusion | flops 3235905536 | bytes 12320776 | tf_op jit(solution)/shard_map/dot_general | solution.py:22
  45.4 0.0 copy-start.3
  45.4 0.0 copy-start.2
  45.4 0.0 copy-start.1
  45.4 0.0 copy-start
  45.4 0.0 reduce-scatter.2.cloned.1.call-update
  45.4 0.6 copy-done.3
  46.1 0.1 broadcast_in_dim.37
  46.2 0.2 reshape.53
  46.4 0.0 copy-done.2
  46.4 0.2 lt.30
  46.6 0.0 copy-done.1
  46.7 17.0 %pmax.21 = f32[2646]{0:T(1024)S(1)} all-reduce(f32[2646]{0:T(1024)S(1)} %broadcast_select_fusion.1), channel_id=1, replica_groups=mesh['dp'=4,'section'=2,'tensor'=4] {'tensor'}, use_global_device_ids=true, to_apply=%region_0.1 | all-reduce | flops 2646 | bytes 21168 | tf_op jit(solution)/shard_map/pmax | solution.py:10
  63.7 8.1 %pmax.22 = f32[2646]{0:T(1024)S(1)} all-reduce(f32[2646]{0:T(1024)S(1)} %pmax.21), channel_id=1, replica_groups=mesh['dp'=4,'section'=2,'tensor'=4] {'section'}, use_global_device_ids=true, to_apply=%region_1.2 | all-reduce | flops 2646 | bytes 21168 | tf_op jit(solution)/shard_map/pmax | solution.py:11
  71.8 11.8 %pmax.23 = f32[2646]{0:T(1024)S(1)} all-reduce(f32[2646]{0:T(1024)S(1)} %pmax.22), channel_id=1, replica_groups=mesh['dp'=4,'section'=2,'tensor'=4] {'dp'}, use_global_device_ids=true, to_apply=%region_2.3 | all-reduce | flops 2646 | bytes 21168 | tf_op jit(solution)/shard_map/pmax | solution.py:12
  83.6 0.0 copy-done
  83.6 2.9 %select_reduce_fusion = (f32[2646]{0:T(1024)S(1)}, f32[128,2646]{0,1:T(8,128)}) fusion(s32[128]{0:T(128)S(1)} %and_select_fusion.1, s32[2646]{0:T(1024)S(1)} %lt.30, f32[128,2646]{0,1:T(8,128)S(1)} %copy-done, f32[2646]{0:T(1024)S(1)} %pmax.23, pred[128]{0:T(512)(128)(4,1)S(1)} %iota_compare_fusion), kind=kLoop, calls=%fused_computation.6 | loop fusion | flops 1352106 | bytes 2741896 | tf_op jit(solution)/shard_map/reduce_max | solution.py:50
  86.4 0.6 broadcast_divide_fusion
  87.1 29.6 %reduce-scatter.2.cloned.1.call-done = bf16[1024,1024]{1,0:T(8,128)(2,1)} async-done(((bf16[4096,1024]{1,0:T(8,128)(2,1)}), bf16[1024,1024]{1,0:T(8,128)(2,1)}) %reduce-scatter.2.cloned.1.call-update) | async-done | bytes 2097168 | tf_op jit(solution)/shard_map/reduce_scatter | solution.py:25
  (8 shorter events, 0.1 us)
Async XLA Ops:
  7.2 109.4 %reduce-scatter.2.cloned.1.call-start = ((), (), s32[]{:S(2)}) async-start(), calls=%async_computation.1 | async-start | bytes 10485760 | tf_op jit(solution)/shard_map/reduce_scatter | solution.py:25
  45.4 0.7 copy-start.3
  45.4 1.0 copy-start.2
  45.4 1.2 copy-start.1
  45.4 38.2 %copy-start = (f32[128,2646]{0,1:T(8,128)S(1)}, f32[128,2646]{0,1:T(8,128)}, u32[]{:S(2)}) copy-start(f32[128,2646]{0,1:T(8,128)} %param.11) | copy-start | bytes 4064260
Sparse Core Ops, SparseCore 0:
  45.6 70.9 reduce-scatter.1
